TPU v7x, 32 devices: a whole 2x2x4 slice. The times are simulated.
32 devices in a mesh: files: 8 (over z, y), rep: 4 (over x, core).
Axes of the slice: x: 2, y: 2, z: 4, core: 2. Of those that a mesh axis runs over, the one named last changes fastest.
Arguments:
- tile_id: int32 [131072], P(('files', 'rep')), may hold values from 0 to 127, as said below
- pix_row: int32 [131072], P(('files', 'rep')), may hold values from 0 to 31
- pix_col: int32 [131072], P(('files', 'rep')), may hold values from 0 to 127
- point_value: bfloat16 [131072], P(('files', 'rep')), may hold values from -6 to 6
Outputs:
- tile_sums: float32 [128, 32, 128], P('files', 'rep')
Inputs may be any that keep to these rules, and one draw needn't show every extreme that they name: `tile_id`: of the points of one device, at most 2048 lie in tiles of one file group (tile id modulo 8), and on every device some group holds exactly 2048 of them.
All inputs are finite; a program needn't handle non-finite values.
Results may differ from a plain program's by a relative error of at most 0.0003.
Values sent between devices are 32-bit elements; how exact they have to be, the bound alone decides.
A program may use at most 64 MiB of HBM per device.

v0:
```python
import functools

import jax
import jax.numpy as jnp
from jax import lax
from jax.experimental import pallas as pl
from jax.experimental.pallas import tpu as pltpu
from jax.sharding import PartitionSpec as P

LANES = 128
WIDE = 256
TR = 32
TILES = 128
JOIN = 2
ORDER = (1, 2, 6, 3, 7, 4, 5)
MESH = pl.DeviceIdType.MESH


def flipped(index, mask, count):
    out = index
    bit = 1
    while bit < count:
        if mask & bit:
            out = out + (1 - 2 * ((index // bit) % 2)) * bit
        bit *= 2
    return out


def kernel(nf, nr, owned, quarter, tile_ref, row_ref, col_ref, val_ref, parts,
           tile_in, row_in, col_in, val_in, got, acc,
           isem, osem, gsend, grecv, rsend, rrecv):
    f = lax.axis_index("files")
    r = lax.axis_index("rep")
    half = owned * quarter // 2
    band = nr * half
    blocks = tile_ref.shape[0]

    loads = []
    for i, (src, dst) in enumerate(((tile_ref, tile_in), (row_ref, row_in), (col_ref, col_in), (val_ref, val_in))):
        load = pltpu.make_async_copy(src, dst, isem.at[i])
        load.start()
        loads.append(load)
    barrier = pltpu.get_barrier_semaphore()
    for k in range(1, nf):
        pl.semaphore_signal(barrier, inc=1, device_id={"files": flipped(f, k, nf)}, device_id_type=MESH)
    for k in range(1, nr):
        pl.semaphore_signal(barrier, inc=1, device_id={"rep": flipped(r, k, nr)}, device_id_type=MESH)

    for load in loads:
        load.wait()
    tile = tile_in[...]
    prow = row_in[...]
    owner = tile % nf
    inner = (tile // nf) * quarter + prow % quarter
    cell = (owner * band + (prow // quarter) * half + inner % half) * WIDE
    cell = cell + (inner // half) * LANES + col_in[...]
    got[0, 0:blocks, :] = cell.astype(jnp.float32)
    got[0, blocks:, :] = val_in[...].astype(jnp.float32)

    pl.semaphore_wait(barrier, nf + nr - 2)

    sends = []
    for i, k in enumerate(ORDER if nf == 8 else range(1, nf), 1):
        copy = pltpu.make_async_remote_copy(
            src_ref=got.at[0], dst_ref=got.at[i], send_sem=gsend.at[i], recv_sem=grecv.at[i],
            device_id={"files": flipped(f, k, nf)}, device_id_type=MESH)
        copy.start()
        sends.append(copy)

    ids16 = lax.broadcasted_iota(jnp.int32, (16, LANES), 0)
    lane = lax.broadcasted_iota(jnp.int32, (LANES, LANES), 1)
    lane_lo = lane.astype(jnp.float32).astype(jnp.bfloat16)
    lane_hi = (lane + LANES).astype(jnp.float32).astype(jnp.bfloat16)
    one = jnp.ones((), jnp.bfloat16)
    zero = jnp.zeros((), jnp.bfloat16)
    first = (f * band).astype(jnp.float32)

    join = min(JOIN, nf)

    def add_points(sets):
        lhs = []
        rhs = []
        for cells, values in sets:
            row = jnp.floor(cells * (1.0 / WIDE))
            col_t = jnp.transpose(cells - row * WIDE)
            row = row - first
            for j in range(blocks):
                row16 = jnp.broadcast_to(row[j:j + 1, :], (16, LANES)).astype(jnp.bfloat16)
                val16 = jnp.broadcast_to(values[j:j + 1, :], (16, LANES)).astype(jnp.bfloat16)
                lhs.append(jnp.concatenate([
                    jnp.where(row16 == (ids16 + 16 * i).astype(jnp.float32).astype(jnp.bfloat16), val16, zero)
                    for i in range(band // 16)], axis=0))
                colb = jnp.broadcast_to(col_t[:, j:j + 1], (LANES, LANES)).astype(jnp.bfloat16)
                rhs.append(jnp.concatenate([
                    jnp.where(colb == lane_lo, one, zero),
                    jnp.where(colb == lane_hi, one, zero)], axis=1))
        total = jnp.dot(jnp.concatenate(lhs, axis=1), jnp.concatenate(rhs, axis=0),
                        preferred_element_type=jnp.float32)
        for q in range(nr):
            block = total[q * half:(q + 1) * half, :]
            acc[q, 0] += block[:, :LANES]
            acc[q, 1] += block[:, LANES:]

    acc[...] = jnp.zeros_like(acc)

    def wait_for(i):
        pltpu.make_async_remote_copy(
            src_ref=got.at[0], dst_ref=got.at[i], send_sem=gsend.at[i], recv_sem=grecv.at[i],
            device_id={"files": (f + 1) % nf}, device_id_type=MESH).wait_recv()

    def step(t, carry):
        pl.when(t > 0)(lambda: wait_for(t * join))
        for i in range(1, join):
            wait_for(t * join + i)
        add_points([(got[t * join + i, 0:blocks, :], got[t * join + i, blocks:, :]) for i in range(join)])
        return carry

    lax.fori_loop(0, nf // join, step, 0)

    backs = []
    for k in tuple(range(2, nr)) + (1,):
        peer = flipped(r, k, nr)
        copy = pltpu.make_async_remote_copy(
            src_ref=acc.at[peer], dst_ref=parts.at[k], send_sem=rsend.at[k], recv_sem=rrecv.at[k],
            device_id={"rep": peer}, device_id_type=MESH)
        copy.start()
        backs.append(copy)
    own = pltpu.make_async_copy(acc.at[r], parts.at[0], osem)
    own.start()
    for copy in sends:
        copy.wait_send()
    own.wait()
    for copy in backs:
        copy.wait()


def solution(mesh):
    nf = mesh.shape["files"]
    nr = mesh.shape["rep"]
    owned = TILES // nf
    quarter = TR // nr
    half = owned * quarter // 2

    def per_device(tile_id, pix_row, pix_col, point_value):
        blocks = tile_id.shape[0] // LANES
        shape = (blocks, LANES)
        out = pl.pallas_call(
            functools.partial(kernel, nf, nr, owned, quarter),
            out_shape=jax.ShapeDtypeStruct((nr, 2, half, LANES), jnp.float32),
            in_specs=[pl.BlockSpec(memory_space=pl.ANY)] * 4,
            out_specs=pl.BlockSpec(memory_space=pl.ANY),
            scratch_shapes=[
                pltpu.VMEM(shape, jnp.int32),
                pltpu.VMEM(shape, jnp.int32),
                pltpu.VMEM(shape, jnp.int32),
                pltpu.VMEM(shape, point_value.dtype),
                pltpu.VMEM((nf, 2 * blocks, LANES), jnp.float32),
                pltpu.VMEM((nr, 2, half, LANES), jnp.float32),
                pltpu.SemaphoreType.DMA((4,)),
                pltpu.SemaphoreType.DMA,
                pltpu.SemaphoreType.DMA((nf,)),
                pltpu.SemaphoreType.DMA((nf,)),
                pltpu.SemaphoreType.DMA((nr,)),
                pltpu.SemaphoreType.DMA((nr,)),
            ],
            compiler_params=pltpu.CompilerParams(collective_id=0, has_side_effects=True),
        )(tile_id.reshape(shape), pix_row.reshape(shape), pix_col.reshape(shape),
          point_value.reshape(shape))
        return jnp.sum(out, axis=0).reshape(owned, quarter, LANES)

    both = P(("files", "rep"))
    return jax.shard_map(per_device, mesh=mesh, in_specs=(both,) * 4,
                         out_specs=P("files", "rep", None), check_vma=False)
```

profile of v0, /device:TPU:0, one launch (start us, length us, event | category | flops | bytes accessed | tf_op | source)
XLA Modules:
  0.0 21.1 jit_solution(2435156293657711699)
XLA Ops:
  0.0 19.4 %shard_map.46 = f32[4,2,64,128]{3,2,1,0:T(8,128)} custom-call(s32[32,128]{1,0:T(8,128)} %bitcast.5, s32[32,128]{1,0:T(8,128)} %bitcast.6, s32[32,128]{1,0:T(8,128)} %bitcast.7, bf16[32,128]{1,0:T(8,128)(2,1)} %bitcast.8), custom_call_target="tpu_custom_call" | custom-call | tf_op jit(solution)/shard_map/pallas_call | solution.py:147
  19.4 1.6 %reduce_sum.9 = f32[2,64,128]{2,1,0:T(8,128)} reduce(f32[4,2,64,128]{3,2,1,0:T(8,128)} %shard_map.46, f32[]{:T(128)} %constant.0.clone.1), dimensions={0}, to_apply=%region_0.0 | reduce | flops 49152 | bytes 327684 | tf_op jit(solution)/shard_map/reduce_sum | solution.py:169
where the time goes:
time: 21.4 us; the launch traced here: 21.1 us
  Pallas kernels  19.4 us (91%)
  other arithmetic  1.6 us (7%)
    pallas_call x1, Pallas kernels, per_device(): pl.pallas_call(functools.partial(kernel, nf, nr, owned, quarter), out_sha...  19.4 us
    reduce_sum x1, other arithmetic, per_device(): return jnp.sum(out, axis=0).reshape(owned, quarter, LANES)  1.6 us

commit v1 on v0

--- a/solution.py
+++ b/solution.py
@@ -11,7 +11,6 @@
 WIDE = 256
 TR = 32
 TILES = 128
-JOIN = 2
 ORDER = (1, 2, 6, 3, 7, 4, 5)
 MESH = pl.DeviceIdType.MESH
 
@@ -67,35 +66,29 @@
         copy.start()
         sends.append(copy)
 
-    ids16 = lax.broadcasted_iota(jnp.int32, (16, LANES), 0)
-    lane = lax.broadcasted_iota(jnp.int32, (LANES, LANES), 1)
-    lane_lo = lane.astype(jnp.float32).astype(jnp.bfloat16)
-    lane_hi = (lane + LANES).astype(jnp.float32).astype(jnp.bfloat16)
+    ids = [(lax.broadcasted_iota(jnp.int32, (16, LANES), 0) + 16 * i).astype(jnp.float32).astype(jnp.bfloat16)
+           for i in range(WIDE // 16)]
     one = jnp.ones((), jnp.bfloat16)
     zero = jnp.zeros((), jnp.bfloat16)
     first = (f * band).astype(jnp.float32)
 
-    join = min(JOIN, nf)
+    def wide(line):
+        return jnp.broadcast_to(line, (16, LANES)).astype(jnp.bfloat16)
 
-    def add_points(sets):
+    def add_points(cells, values):
+        row = jnp.floor(cells * (1.0 / WIDE))
+        col = cells - row * WIDE
+        row = row - first
         lhs = []
         rhs = []
-        for cells, values in sets:
-            row = jnp.floor(cells * (1.0 / WIDE))
-            col_t = jnp.transpose(cells - row * WIDE)
-            row = row - first
-            for j in range(blocks):
-                row16 = jnp.broadcast_to(row[j:j + 1, :], (16, LANES)).astype(jnp.bfloat16)
-                val16 = jnp.broadcast_to(values[j:j + 1, :], (16, LANES)).astype(jnp.bfloat16)
-                lhs.append(jnp.concatenate([
-                    jnp.where(row16 == (ids16 + 16 * i).astype(jnp.float32).astype(jnp.bfloat16), val16, zero)
-                    for i in range(band // 16)], axis=0))
-                colb = jnp.broadcast_to(col_t[:, j:j + 1], (LANES, LANES)).astype(jnp.bfloat16)
-                rhs.append(jnp.concatenate([
-                    jnp.where(colb == lane_lo, one, zero),
-                    jnp.where(colb == lane_hi, one, zero)], axis=1))
-        total = jnp.dot(jnp.concatenate(lhs, axis=1), jnp.concatenate(rhs, axis=0),
-                        preferred_element_type=jnp.float32)
+        for j in range(blocks):
+            row16 = wide(row[j:j + 1, :])
+            col16 = wide(col[j:j + 1, :])
+            val16 = wide(values[j:j + 1, :])
+            lhs.append(jnp.concatenate([jnp.where(row16 == ids[i], val16, zero) for i in range(band // 16)], axis=0))
+            rhs.append(jnp.concatenate([jnp.where(col16 == ids[i], one, zero) for i in range(WIDE // 16)], axis=0))
+        total = lax.dot_general(jnp.concatenate(lhs, axis=1), jnp.concatenate(rhs, axis=1),
+                                (((1,), (1,)), ((), ())), preferred_element_type=jnp.float32)
         for q in range(nr):
             block = total[q * half:(q + 1) * half, :]
             acc[q, 0] += block[:, :LANES]
@@ -109,13 +102,11 @@
             device_id={"files": (f + 1) % nf}, device_id_type=MESH).wait_recv()
 
     def step(t, carry):
-        pl.when(t > 0)(lambda: wait_for(t * join))
-        for i in range(1, join):
-            wait_for(t * join + i)
-        add_points([(got[t * join + i, 0:blocks, :], got[t * join + i, blocks:, :]) for i in range(join)])
+        pl.when(t > 0)(lambda: wait_for(t))
+        add_points(got[t, 0:blocks, :], got[t, blocks:, :])
         return carry
 
-    lax.fori_loop(0, nf // join, step, 0)
+    lax.fori_loop(0, nf, step, 0)
 
     backs = []
     for k in tuple(range(2, nr)) + (1,):

time: 21.4 us -> 19.8 us (0.925)
  Pallas kernels: 19.4 us -> 17.9 us
    pallas_call x1, Pallas kernels: 19.4 us -> 17.9 us  [per_device(): pl.pallas_call(functools.partial(kernel, nf, nr, owned, quarter), out_sha...]
where the time goes in v1:
time: 19.8 us; the launch traced here: 19.5 us
  Pallas kernels  17.9 us (90%)
  other arithmetic  1.6 us (8%)
    pallas_call x1, Pallas kernels, per_device(): pl.pallas_call(functools.partial(kernel, nf, nr, owned, quarter), out_sha...  17.9 us
    reduce_sum x1, other arithmetic, per_device(): return jnp.sum(out, axis=0).reshape(owned, quarter, LANES)  1.6 us

profile of v1, /device:TPU:0, one launch (start us, length us, event | category | flops | bytes accessed | tf_op | source)
XLA Modules:
  0.0 19.5 jit_solution(17992474676870440441)
XLA Ops:
  0.0 17.9 %shard_map.46 = f32[4,2,64,128]{3,2,1,0:T(8,128)} custom-call(s32[32,128]{1,0:T(8,128)} %bitcast.5, s32[32,128]{1,0:T(8,128)} %bitcast.6, s32[32,128]{1,0:T(8,128)} %bitcast.7, bf16[32,128]{1,0:T(8,128)(2,1)} %bitcast.8), custom_call_target="tpu_custom_call" | custom-call | tf_op jit(solution)/shard_map/pallas_call | solution.py:138
  17.9 1.6 %reduce_sum.9 = f32[2,64,128]{2,1,0:T(8,128)} reduce(f32[4,2,64,128]{3,2,1,0:T(8,128)} %shard_map.46, f32[]{:T(128)} %constant.0.clone.1), dimensions={0}, to_apply=%region_0.0 | reduce | flops 49152 | bytes 327684 | tf_op jit(solution)/shard_map/reduce_sum | solution.py:160

commit v2 on v1

--- a/solution.py
+++ b/solution.py
@@ -25,8 +25,8 @@
     return out
 
 
-def kernel(nf, nr, owned, quarter, tile_ref, row_ref, col_ref, val_ref, parts,
-           tile_in, row_in, col_in, val_in, got, acc,
+def kernel(nf, nr, owned, quarter, tile_ref, row_ref, col_ref, val_ref, out,
+           tile_in, row_in, col_in, val_in, got, acc, parts,
            isem, osem, gsend, grecv, rsend, rrecv):
     f = lax.axis_index("files")
     r = lax.axis_index("rep")
@@ -116,13 +116,14 @@
             device_id={"rep": peer}, device_id_type=MESH)
         copy.start()
         backs.append(copy)
-    own = pltpu.make_async_copy(acc.at[r], parts.at[0], osem)
-    own.start()
     for copy in sends:
         copy.wait_send()
-    own.wait()
     for copy in backs:
         copy.wait()
+    tot = acc[r]
+    for k in range(1, nr):
+        tot = tot + parts[k]
+    out[...] = tot.reshape(out.shape)
 
 
 def solution(mesh):
@@ -137,15 +138,16 @@
         shape = (blocks, LANES)
         out = pl.pallas_call(
             functools.partial(kernel, nf, nr, owned, quarter),
-            out_shape=jax.ShapeDtypeStruct((nr, 2, half, LANES), jnp.float32),
+            out_shape=jax.ShapeDtypeStruct((2 * half, LANES), jnp.float32),
             in_specs=[pl.BlockSpec(memory_space=pl.ANY)] * 4,
-            out_specs=pl.BlockSpec(memory_space=pl.ANY),
+            out_specs=pl.BlockSpec(memory_space=pltpu.VMEM),
             scratch_shapes=[
                 pltpu.VMEM(shape, jnp.int32),
                 pltpu.VMEM(shape, jnp.int32),
                 pltpu.VMEM(shape, jnp.int32),
                 pltpu.VMEM(shape, point_value.dtype),
                 pltpu.VMEM((nf, 2 * blocks, LANES), jnp.float32),
+                pltpu.VMEM((nr, 2, half, LANES), jnp.float32),
                 pltpu.VMEM((nr, 2, half, LANES), jnp.float32),
                 pltpu.SemaphoreType.DMA((4,)),
                 pltpu.SemaphoreType.DMA,
@@ -154,10 +156,10 @@
                 pltpu.SemaphoreType.DMA((nr,)),
                 pltpu.SemaphoreType.DMA((nr,)),
             ],
-            compiler_params=pltpu.CompilerParams(collective_id=0, has_side_effects=True),
-        )(tile_id.reshape(shape), pix_row.reshape(shape), pix_col.reshape(shape),
-          point_value.reshape(shape))
-        return jnp.sum(out, axis=0).reshape(owned, quarter, LANES)
+            compiler_params=pltpu.CompilerParams(collective_id=0, has_side_effects=True, vmem_limit_bytes=12*1024*1024),
+        )(*[pltpu.with_memory_space_constraint(x.reshape(shape), pltpu.HBM)
+            for x in (tile_id, pix_row, pix_col, point_value)])
+        return out.reshape(owned, quarter, LANES)
 
     both = P(("files", "rep"))
     return jax.shard_map(per_device, mesh=mesh, in_specs=(both,) * 4,

time: 19.8 us -> 18.7 us (0.944)
  other arithmetic: 1.6 us -> 0 us
  local copies, waits for them, and re-layouts: 0 us -> 0.63 us
    reduce_sum x1 -> x0, other arithmetic: 1.6 us -> none  [per_device(): return jnp.sum(out, axis=0).reshape(owned, quarter, LANES)]
    unnamed x0 -> x1, local copies, waits for them, and re-layouts: none -> 0.63 us
where the time goes in v2:
time: 18.7 us; the launch traced here: 18.4 us
  Pallas kernels  17.8 us (95%)
  local copies, waits for them, and re-layouts  0.63 us (3%)
    pallas_call x1, Pallas kernels, per_device(): pl.pallas_call(functools.partial(kernel, nf, nr, owned, quarter), out_sha...  17.8 us
    unnamed x1, local copies, waits for them, and re-layouts  0.63 us

profile of v2, /device:TPU:0, one launch (start us, length us, event | category | flops | bytes accessed | tf_op | source)
XLA Modules:
  0.0 18.4 jit_solution(3813463365999848375)
XLA Ops:
  0.0 17.8 %shard_map.46 = f32[128,128]{1,0:T(8,128)S(1)} custom-call(s32[32,128]{1,0:T(8,128)} %bitcast.6, s32[32,128]{1,0:T(8,128)} %bitcast.7, s32[32,128]{1,0:T(8,128)} %bitcast.8, bf16[32,128]{1,0:T(8,128)(2,1)} %bitcast.9), custom_call_target="tpu_custom_call" | custom-call | tf_op jit(solution)/shard_map/pallas_call | solution.py:139
  17.8 0.6 %copy.6 = f32[16,8,128]{2,1,0:T(8,128)} copy(f32[16,8,128]{2,1,0:T(8,128)S(1)} %bitcast.5) | data formatting | bytes 131072

commit v3 on v2

v3 whole, which is shorter than its diff:
```python
import functools

import jax
import jax.numpy as jnp
from jax import lax
from jax.experimental import pallas as pl
from jax.experimental.pallas import tpu as pltpu
from jax.sharding import PartitionSpec as P

LANES = 128
WIDE = 256
TR = 32
TILES = 128
SLACK = 4
ORDER = (7, 6, 5, 4, 3, 2, 1)
ARRIVE = (1, 2, 3, 6, 4, 7, 5)
MESH = pl.DeviceIdType.MESH
BF16 = jnp.bfloat16


def flipped(index, mask, count):
    out = index
    bit = 1
    while bit < count:
        if mask & bit:
            out = out + (1 - 2 * ((index // bit) % 2)) * bit
        bit *= 2
    return out


def iota(shape, dim):
    return lax.broadcasted_iota(jnp.int32, shape, dim)


def dot(a, b, transposed=False):
    return lax.dot_general(a, b, (((1,), (1 if transposed else 0,)), ((), ())),
                           preferred_element_type=jnp.float32)


def kernel(nf, nr, owned, quarter, cap, tile_ref, row_ref, col_ref, val_ref, out,
           tile_in, row_in, col_in, val_in, packed, got, acc, parts,
           isem, gsend, grecv, rsend, rrecv):
    f = lax.axis_index("files")
    r = lax.axis_index("rep")
    half = owned * quarter // 2
    band = nr * half
    blocks = tile_ref.shape[0]
    width = min(WIDE, cap)
    lines = cap // width
    slots = nf * lines
    rows = cap // LANES

    loads = []
    for i, (src, dst) in enumerate(((tile_ref, tile_in), (row_ref, row_in), (col_ref, col_in), (val_ref, val_in))):
        load = pltpu.make_async_copy(src, dst, isem.at[i])
        load.start()
        loads.append(load)
    barrier = pltpu.get_barrier_semaphore()
    for k in range(1, nf):
        pl.semaphore_signal(barrier, inc=1, device_id={"files": flipped(f, k, nf)}, device_id_type=MESH)
    for k in range(1, nr):
        pl.semaphore_signal(barrier, inc=1, device_id={"rep": flipped(r, k, nr)}, device_id_type=MESH)

    one = jnp.ones((), BF16)
    zero = jnp.zeros((), BF16)
    ids = [(iota((16, LANES), 0) + 16 * i).astype(jnp.float32).astype(BF16) for i in range(WIDE // 16)]
    upto = jnp.where(iota((LANES, 2 * LANES), 0) <= iota((LANES, 2 * LANES), 1), 1.0, 0.0).astype(BF16)
    group = max(1, WIDE // blocks)
    span = group * blocks
    i0 = iota((span, span), 0)
    i1 = iota((span, span), 1)
    above = jnp.where((i1 < i0) & (i1 // blocks == i0 // blocks), 1.0, 0.0).astype(BF16)
    acc[...] = jnp.zeros_like(acc)

    for load in loads:
        load.wait()
    tile = tile_in[...]
    prow = row_in[...]
    owner = tile % nf
    inner = (tile // nf) * quarter + prow % quarter
    place = ((prow // quarter) * half + inner % half).astype(jnp.float32)
    col = ((inner // half) * LANES + col_in[...]).astype(jnp.float32)
    values = val_in[...].astype(jnp.float32)

    rank = jnp.zeros((blocks, LANES), jnp.float32)
    for g in range(0, nf, group):
        mine = [owner == o for o in range(g, g + group)]
        marks = jnp.concatenate([jnp.where(m, 1.0, 0.0) for m in mine], axis=0).astype(BF16)
        run = dot(marks, upto)
        before = dot(above, run[:, LANES:].astype(BF16))
        full = run[:, :LANES] + before - 1.0
        for i, m in enumerate(mine):
            rank = rank + jnp.where(m, full[i * blocks:(i + 1) * blocks, :], 0.0)
    slot = owner.astype(jnp.float32) * cap + rank
    line = jnp.floor(slot * (1.0 / width))
    at = slot - line * width

    def wide(x):
        return jnp.broadcast_to(x, (16, LANES)).astype(BF16)

    def one_hot(x, count, payloads):
        picks = [x == ids[i] for i in range(count // 16)]
        return [jnp.concatenate([jnp.where(m, p, zero) for m in picks], axis=0) for p in payloads]

    lhs = []
    rhs = []
    for j in range(blocks):
        pick = [wide(x[j:j + 1, :]) for x in (line, at, place, col, values)]
        lhs.append(jnp.concatenate(one_hot(pick[0], slots, pick[2:]), axis=0))
        rhs.append(one_hot(pick[1], width, [one])[0])
    moved = dot(jnp.concatenate(lhs, axis=1), jnp.concatenate(rhs, axis=1), True)
    cells = moved[:slots] * WIDE + moved[slots:2 * slots]
    vals = moved[2 * slots:]
    for o in range(nf):
        for h in range(width // LANES):
            piece = (slice(o * lines, (o + 1) * lines), slice(h * LANES, (h + 1) * LANES))
            packed[o, h * lines:(h + 1) * lines, :] = cells[piece]
            packed[o, rows + h * lines:rows + (h + 1) * lines, :] = vals[piece]

    pl.semaphore_wait(barrier, nf + nr - 2)

    sends = []
    for k in ORDER if nf == 8 else range(1, nf):
        to = flipped(f, k, nf)
        copy = pltpu.make_async_remote_copy(
            src_ref=packed.at[to], dst_ref=got.at[k], send_sem=gsend.at[k], recv_sem=grecv.at[k],
            device_id={"files": to}, device_id_type=MESH)
        copy.start()
        sends.append(copy)

    def add_points(cells, values):
        row = jnp.floor(cells * (1.0 / WIDE))
        col = cells - row * WIDE
        lhs = []
        rhs = []
        for j in range(rows):
            row16, col16, val16 = [wide(x[j:j + 1, :]) for x in (row, col, values)]
            lhs.append(one_hot(row16, band, [val16])[0])
            rhs.append(one_hot(col16, WIDE, [one])[0])
        total = dot(jnp.concatenate(lhs, axis=1), jnp.concatenate(rhs, axis=1), True)
        for q in range(nr):
            block = total[q * half:(q + 1) * half, :]
            acc[q, 0] += block[:, :LANES]
            acc[q, 1] += block[:, LANES:]

    add_points(packed[f, 0:rows, :], packed[f, rows:, :])

    def step(t, carry):
        k = t
        if nf == 8:
            k = sum(jnp.where(t == i, mask, 0) for i, mask in enumerate(ARRIVE, 1))
        pltpu.make_async_remote_copy(
            src_ref=packed.at[0], dst_ref=got.at[k], send_sem=gsend.at[k], recv_sem=grecv.at[k],
            device_id={"files": (f + 1) % nf}, device_id_type=MESH).wait_recv()
        add_points(got[k, 0:rows, :], got[k, rows:, :])
        return carry

    lax.fori_loop(1, nf, step, 0)

    backs = []
    for k in tuple(range(2, nr)) + (1,):
        peer = flipped(r, k, nr)
        copy = pltpu.make_async_remote_copy(
            src_ref=acc.at[peer], dst_ref=parts.at[k], send_sem=rsend.at[k], recv_sem=rrecv.at[k],
            device_id={"rep": peer}, device_id_type=MESH)
        copy.start()
        backs.append(copy)
    for copy in sends:
        copy.wait_send()
    for copy in backs:
        copy.wait()
    total = acc[r]
    for k in range(1, nr):
        total = total + parts[k]
    out[...] = total.reshape(out.shape)


def solution(mesh):
    nf = mesh.shape["files"]
    nr = mesh.shape["rep"]
    owned = TILES // nf
    quarter = TR // nr
    half = owned * quarter // 2

    def per_device(tile_id, pix_row, pix_col, point_value):
        points = tile_id.shape[0]
        cap = SLACK * points // nf
        shape = (points // LANES, LANES)
        message = 2 * cap // LANES
        out = pl.pallas_call(
            functools.partial(kernel, nf, nr, owned, quarter, cap),
            out_shape=jax.ShapeDtypeStruct((2 * half, LANES), jnp.float32),
            in_specs=[pl.BlockSpec(memory_space=pl.ANY)] * 4,
            out_specs=pl.BlockSpec(memory_space=pltpu.VMEM),
            scratch_shapes=[
                pltpu.VMEM(shape, jnp.int32),
                pltpu.VMEM(shape, jnp.int32),
                pltpu.VMEM(shape, jnp.int32),
                pltpu.VMEM(shape, point_value.dtype),
                pltpu.VMEM((nf, message, LANES), jnp.float32),
                pltpu.VMEM((nf, message, LANES), jnp.float32),
                pltpu.VMEM((nr, 2, half, LANES), jnp.float32),
                pltpu.VMEM((nr, 2, half, LANES), jnp.float32),
                pltpu.SemaphoreType.DMA((4,)),
                pltpu.SemaphoreType.DMA((nf,)),
                pltpu.SemaphoreType.DMA((nf,)),
                pltpu.SemaphoreType.DMA((nr,)),
                pltpu.SemaphoreType.DMA((nr,)),
            ],
            compiler_params=pltpu.CompilerParams(collective_id=0, has_side_effects=True,
                                                 vmem_limit_bytes=16 * 1024 * 1024),
        )(*[pltpu.with_memory_space_constraint(x.reshape(shape), pltpu.HBM)
            for x in (tile_id, pix_row, pix_col, point_value)])
        return out.reshape(owned, quarter, LANES)

    both = P(("files", "rep"))
    return jax.shard_map(per_device, mesh=mesh, in_specs=(both,) * 4,
                         out_specs=P("files", "rep", None), check_vma=False)
```

time: 18.7 us -> 17 us (0.909)
  Pallas kernels: 17.8 us -> 16.1 us
    pallas_call x1, Pallas kernels: 17.8 us -> 16.1 us  [per_device(): pl.pallas_call(functools.partial(kernel, nf, nr, owned, quarter, cap), ou...]
where the time goes in v3:
time: 17 us; the launch traced here: 16.7 us
  Pallas kernels  16.1 us (95%)
  local copies, waits for them, and re-layouts  0.63 us (4%)
    pallas_call x1, Pallas kernels, per_device(): pl.pallas_call(functools.partial(kernel, nf, nr, owned, quarter, cap), ou...  16.1 us
    unnamed x1, local copies, waits for them, and re-layouts  0.63 us

profile of v3, /device:TPU:0, one launch (start us, length us, event | category | flops | bytes accessed | tf_op | source)
XLA Modules:
  0.0 16.7 jit_solution(13485224783117288481)
XLA Ops:
  0.0 16.1 %shard_map.46 = f32[128,128]{1,0:T(8,128)S(1)} custom-call(s32[32,128]{1,0:T(8,128)} %bitcast.6, s32[32,128]{1,0:T(8,128)} %bitcast.7, s32[32,128]{1,0:T(8,128)} %bitcast.8, bf16[32,128]{1,0:T(8,128)(2,1)} %bitcast.9), custom_call_target="tpu_custom_call" | custom-call | tf_op jit(solution)/shard_map/pallas_call | solution.py:190
  16.1 0.6 %copy.6 = f32[16,8,128]{2,1,0:T(8,128)} copy(f32[16,8,128]{2,1,0:T(8,128)S(1)} %bitcast.5) | data formatting | bytes 131072

commit v4 on v3

--- a/solution.py
+++ b/solution.py
@@ -12,8 +12,6 @@
 TR = 32
 TILES = 128
 SLACK = 4
-ORDER = (7, 6, 5, 4, 3, 2, 1)
-ARRIVE = (1, 2, 3, 6, 4, 7, 5)
 MESH = pl.DeviceIdType.MESH
 BF16 = jnp.bfloat16
 
@@ -39,7 +37,7 @@
 
 def kernel(nf, nr, owned, quarter, cap, tile_ref, row_ref, col_ref, val_ref, out,
            tile_in, row_in, col_in, val_in, packed, got, acc, parts,
-           isem, gsend, grecv, rsend, rrecv):
+           isem, fready, rready, gsend, grecv, rsend, rrecv):
     f = lax.axis_index("files")
     r = lax.axis_index("rep")
     half = owned * quarter // 2
@@ -56,10 +54,19 @@
         load.start()
         loads.append(load)
     barrier = pltpu.get_barrier_semaphore()
-    for k in range(1, nf):
-        pl.semaphore_signal(barrier, inc=1, device_id={"files": flipped(f, k, nf)}, device_id_type=MESH)
-    for k in range(1, nr):
-        pl.semaphore_signal(barrier, inc=1, device_id={"rep": flipped(r, k, nr)}, device_id_type=MESH)
+
+    def signal(sem, axis, to):
+        pl.semaphore_signal(sem, inc=1, device_id={axis: to}, device_id_type=MESH)
+
+    for i in range(1, nf):
+        pl.when(f + i < nf)(functools.partial(signal, barrier, "files", f + i))
+    for i in range(1, nr):
+        pl.when(r + i < nr)(functools.partial(signal, barrier, "rep", r + i))
+    pl.when(f + r > 0)(functools.partial(pl.semaphore_wait, barrier, f + r))
+    for i in range(1, nf):
+        pl.when(f - i >= 0)(functools.partial(signal, fready.at[f], "files", f - i))
+    for i in range(1, nr):
+        pl.when(r - i >= 0)(functools.partial(signal, rready.at[r], "rep", r - i))
 
     one = jnp.ones((), BF16)
     zero = jnp.zeros((), BF16)
@@ -117,46 +124,67 @@
             packed[o, h * lines:(h + 1) * lines, :] = cells[piece]
             packed[o, rows + h * lines:rows + (h + 1) * lines, :] = vals[piece]
 
-    pl.semaphore_wait(barrier, nf + nr - 2)
-
-    sends = []
-    for k in ORDER if nf == 8 else range(1, nf):
-        to = flipped(f, k, nf)
-        copy = pltpu.make_async_remote_copy(
-            src_ref=packed.at[to], dst_ref=got.at[k], send_sem=gsend.at[k], recv_sem=grecv.at[k],
+    def send(to):
+        return pltpu.make_async_remote_copy(
+            src_ref=packed.at[to], dst_ref=got.at[f], send_sem=gsend.at[to], recv_sem=grecv.at[f],
             device_id={"files": to}, device_id_type=MESH)
-        copy.start()
-        sends.append(copy)
-
-    def add_points(cells, values):
-        row = jnp.floor(cells * (1.0 / WIDE))
-        col = cells - row * WIDE
+
+    def receive(source):
+        return pltpu.make_async_remote_copy(
+            src_ref=packed.at[f], dst_ref=got.at[source], send_sem=gsend.at[f], recv_sem=grecv.at[source],
+            device_id={"files": source}, device_id_type=MESH)
+
+    for to in range(nf - 1):
+        pl.when(to < f)(lambda to=to: send(to).start())
+
+    def add_points(chunks):
         lhs = []
         rhs = []
-        for j in range(rows):
-            row16, col16, val16 = [wide(x[j:j + 1, :]) for x in (row, col, values)]
-            lhs.append(one_hot(row16, band, [val16])[0])
-            rhs.append(one_hot(col16, WIDE, [one])[0])
+        for chunk in chunks:
+            cells = chunk[0:rows, :]
+            row = jnp.floor(cells * (1.0 / WIDE))
+            col = cells - row * WIDE
+            for j in range(rows):
+                row16, col16, val16 = [wide(x[j:j + 1, :]) for x in (row, col, chunk[rows:, :])]
+                lhs.append(one_hot(row16, band, [val16])[0])
+                rhs.append(one_hot(col16, WIDE, [one])[0])
         total = dot(jnp.concatenate(lhs, axis=1), jnp.concatenate(rhs, axis=1), True)
         for q in range(nr):
             block = total[q * half:(q + 1) * half, :]
             acc[q, 0] += block[:, :LANES]
             acc[q, 1] += block[:, LANES:]
 
-    add_points(packed[f, 0:rows, :], packed[f, rows:, :])
+    got[f] = packed[f]
+
+    for i in range(1, nf):
+        @pl.when(f + i < nf)
+        def _():
+            pl.semaphore_wait(fready.at[f + i], 1)
+            send(f + i).start()
+
+    def arrived(k):
+        source = f
+        bit = 1
+        while bit < nf:
+            source = source + (1 - 2 * ((f // bit) % 2)) * bit * ((k // bit) % 2)
+            bit *= 2
+        pl.when(k > 0)(lambda: receive(source).wait_recv())
+        return source
 
     def step(t, carry):
-        k = t
+        k = 2 * t
         if nf == 8:
-            k = sum(jnp.where(t == i, mask, 0) for i, mask in enumerate(ARRIVE, 1))
-        pltpu.make_async_remote_copy(
-            src_ref=packed.at[0], dst_ref=got.at[k], send_sem=gsend.at[k], recv_sem=grecv.at[k],
-            device_id={"files": (f + 1) % nf}, device_id_type=MESH).wait_recv()
-        add_points(got[k, 0:rows, :], got[k, rows:, :])
+            k = k + jnp.where(((f // 2) % 3 > 0) & (t >= 2), 2 - 4 * (t % 2), 0)
+        pair = [arrived(k), arrived(k + 1)]
+        add_points([got[source] for source in pair])
         return carry
 
-    lax.fori_loop(1, nf, step, 0)
-
+    lax.fori_loop(0, nf // 2, step, 0)
+
+    for i in range(1, nr):
+        @pl.when(r + i < nr)
+        def _():
+            pl.semaphore_wait(rready.at[r + i], 1)
     backs = []
     for k in tuple(range(2, nr)) + (1,):
         peer = flipped(r, k, nr)
@@ -165,8 +193,8 @@
             device_id={"rep": peer}, device_id_type=MESH)
         copy.start()
         backs.append(copy)
-    for copy in sends:
-        copy.wait_send()
+    for to in range(nf):
+        pl.when(to != f)(lambda to=to: send(to).wait_send())
     for copy in backs:
         copy.wait()
     total = acc[r]
@@ -202,6 +230,8 @@
                 pltpu.VMEM((nr, 2, half, LANES), jnp.float32),
                 pltpu.VMEM((nr, 2, half, LANES), jnp.float32),
                 pltpu.SemaphoreType.DMA((4,)),
+                pltpu.SemaphoreType.REGULAR((nf,)),
+                pltpu.SemaphoreType.REGULAR((nr,)),
                 pltpu.SemaphoreType.DMA((nf,)),
                 pltpu.SemaphoreType.DMA((nf,)),
                 pltpu.SemaphoreType.DMA((nr,)),

time: 17 us -> 15.7 us (0.924)
  Pallas kernels: 16.1 us -> 14.8 us
    pallas_call x1, Pallas kernels: 16.1 us -> 14.8 us  [per_device(): pl.pallas_call(functools.partial(kernel, nf, nr, owned, quarter, cap), ou...]
where the time goes in v4:
time: 15.7 us; the launch traced here: 15.4 us
  Pallas kernels  14.8 us (94%)
  local copies, waits for them, and re-layouts  0.63 us (4%)
    pallas_call x1, Pallas kernels, per_device(): pl.pallas_call(functools.partial(kernel, nf, nr, owned, quarter, cap), ou...  14.8 us
    unnamed x1, local copies, waits for them, and re-layouts  0.63 us

profile of v4, /device:TPU:0, one launch (start us, length us, event | category | flops | bytes accessed | tf_op | source)
XLA Modules:
  0.0 15.4 jit_solution(7289027406140622527)
XLA Ops:
  0.0 14.8 %shard_map.46 = f32[128,128]{1,0:T(8,128)S(1)} custom-call(s32[32,128]{1,0:T(8,128)} %bitcast.6, s32[32,128]{1,0:T(8,128)} %bitcast.7, s32[32,128]{1,0:T(8,128)} %bitcast.8, bf16[32,128]{1,0:T(8,128)(2,1)} %bitcast.9), custom_call_target="tpu_custom_call" | custom-call | tf_op jit(solution)/shard_map/pallas_call | solution.py:218
  14.8 0.6 %copy.6 = f32[16,8,128]{2,1,0:T(8,128)} copy(f32[16,8,128]{2,1,0:T(8,128)S(1)} %bitcast.5) | data formatting | bytes 131072

commit v5 on v4

--- a/solution.py
+++ b/solution.py
@@ -12,6 +12,7 @@
 TR = 32
 TILES = 128
 SLACK = 4
+PAIRS = ((0, 2, 4, 6), (0, 2, 6, 4), (0, 6, 2, 4), (0, 2, 4, 6))
 MESH = pl.DeviceIdType.MESH
 BF16 = jnp.bfloat16
 
@@ -35,9 +36,9 @@
                            preferred_element_type=jnp.float32)
 
 
-def kernel(nf, nr, owned, quarter, cap, tile_ref, row_ref, col_ref, val_ref, out,
-           tile_in, row_in, col_in, val_in, packed, got, acc, parts,
-           isem, fready, rready, gsend, grecv, rsend, rrecv):
+def kernel(nf, nr, owned, quarter, cap, tile_ref, row_ref, col_ref, val_ref, parts,
+           tile_in, row_in, col_in, val_in, packed, got, acc,
+           fready, rready, gsend, grecv, rsend, rrecv):
     f = lax.axis_index("files")
     r = lax.axis_index("rep")
     half = owned * quarter // 2
@@ -50,7 +51,7 @@
 
     loads = []
     for i, (src, dst) in enumerate(((tile_ref, tile_in), (row_ref, row_in), (col_ref, col_in), (val_ref, val_in))):
-        load = pltpu.make_async_copy(src, dst, isem.at[i])
+        load = pltpu.make_async_copy(src, dst, rsend.at[i])
         load.start()
         loads.append(load)
     barrier = pltpu.get_barrier_semaphore()
@@ -62,11 +63,14 @@
         pl.when(f + i < nf)(functools.partial(signal, barrier, "files", f + i))
     for i in range(1, nr):
         pl.when(r + i < nr)(functools.partial(signal, barrier, "rep", r + i))
-    pl.when(f + r > 0)(functools.partial(pl.semaphore_wait, barrier, f + r))
-    for i in range(1, nf):
-        pl.when(f - i >= 0)(functools.partial(signal, fready.at[f], "files", f - i))
-    for i in range(1, nr):
-        pl.when(r - i >= 0)(functools.partial(signal, rready.at[r], "rep", r - i))
+    def enter():
+        pl.when(f + r > 0)(functools.partial(pl.semaphore_wait, barrier, f + r))
+        for i in range(1, nf):
+            pl.when(f - i >= 0)(functools.partial(signal, fready.at[f // 2], "files", f - i))
+        for i in range(1, nr):
+            pl.when(r - i >= 0)(functools.partial(signal, rready, "rep", r - i))
+
+    pl.when(f >= nf - 2)(enter)
 
     one = jnp.ones((), BF16)
     zero = jnp.zeros((), BF16)
@@ -98,6 +102,7 @@
         full = run[:, :LANES] + before - 1.0
         for i, m in enumerate(mine):
             rank = rank + jnp.where(m, full[i * blocks:(i + 1) * blocks, :], 0.0)
+    pl.when(f < nf - 2)(enter)
     slot = owner.astype(jnp.float32) * cap + rank
     line = jnp.floor(slot * (1.0 / width))
     at = slot - line * width
@@ -126,12 +131,12 @@
 
     def send(to):
         return pltpu.make_async_remote_copy(
-            src_ref=packed.at[to], dst_ref=got.at[f], send_sem=gsend.at[to], recv_sem=grecv.at[f],
+            src_ref=packed.at[to], dst_ref=got.at[f], send_sem=gsend, recv_sem=grecv.at[f],
             device_id={"files": to}, device_id_type=MESH)
 
     def receive(source):
         return pltpu.make_async_remote_copy(
-            src_ref=packed.at[f], dst_ref=got.at[source], send_sem=gsend.at[f], recv_sem=grecv.at[source],
+            src_ref=packed.at[f], dst_ref=got.at[source], send_sem=gsend, recv_sem=grecv.at[source],
             device_id={"files": source}, device_id_type=MESH)
 
     for to in range(nf - 1):
@@ -156,11 +161,17 @@
 
     got[f] = packed[f]
 
-    for i in range(1, nf):
-        @pl.when(f + i < nf)
+    @pl.when(f % 2 == 0)
+    def _():
+        pl.semaphore_wait(fready.at[f // 2], 1)
+        send(f + 1).start()
+
+    for i in range(1, nf // 2):
+        @pl.when(f // 2 + i < nf // 2)
         def _():
-            pl.semaphore_wait(fready.at[f + i], 1)
-            send(f + i).start()
+            pl.semaphore_wait(fready.at[f // 2 + i], 2)
+            send((f // 2 + i) * 2).start()
+            send((f // 2 + i) * 2 + 1).start()
 
     def arrived(k):
         source = f
@@ -174,17 +185,15 @@
     def step(t, carry):
         k = 2 * t
         if nf == 8:
-            k = k + jnp.where(((f // 2) % 3 > 0) & (t >= 2), 2 - 4 * (t % 2), 0)
+            k = sum(jnp.where((f // 2 == z) & (t == i), first, 0)
+                    for z, order in enumerate(PAIRS) for i, first in enumerate(order))
         pair = [arrived(k), arrived(k + 1)]
         add_points([got[source] for source in pair])
         return carry
 
     lax.fori_loop(0, nf // 2, step, 0)
 
-    for i in range(1, nr):
-        @pl.when(r + i < nr)
-        def _():
-            pl.semaphore_wait(rready.at[r + i], 1)
+    pl.when(r < nr - 1)(functools.partial(pl.semaphore_wait, rready, nr - 1 - r))
     backs = []
     for k in tuple(range(2, nr)) + (1,):
         peer = flipped(r, k, nr)
@@ -193,14 +202,12 @@
             device_id={"rep": peer}, device_id_type=MESH)
         copy.start()
         backs.append(copy)
-    for to in range(nf):
-        pl.when(to != f)(lambda to=to: send(to).wait_send())
+    parts[0] = acc[r]
+    pltpu.make_async_remote_copy(
+        src_ref=packed.at[pl.ds(0, nf - 1)], dst_ref=got.at[pl.ds(0, nf - 1)], send_sem=gsend, recv_sem=grecv.at[0],
+        device_id={"files": f}, device_id_type=MESH).wait_send()
     for copy in backs:
         copy.wait()
-    total = acc[r]
-    for k in range(1, nr):
-        total = total + parts[k]
-    out[...] = total.reshape(out.shape)
 
 
 def solution(mesh):
@@ -217,7 +224,7 @@
         message = 2 * cap // LANES
         out = pl.pallas_call(
             functools.partial(kernel, nf, nr, owned, quarter, cap),
-            out_shape=jax.ShapeDtypeStruct((2 * half, LANES), jnp.float32),
+            out_shape=jax.ShapeDtypeStruct((nr, 2, half, LANES), jnp.float32),
             in_specs=[pl.BlockSpec(memory_space=pl.ANY)] * 4,
             out_specs=pl.BlockSpec(memory_space=pltpu.VMEM),
             scratch_shapes=[
@@ -228,20 +235,18 @@
                 pltpu.VMEM((nf, message, LANES), jnp.float32),
                 pltpu.VMEM((nf, message, LANES), jnp.float32),
                 pltpu.VMEM((nr, 2, half, LANES), jnp.float32),
-                pltpu.VMEM((nr, 2, half, LANES), jnp.float32),
-                pltpu.SemaphoreType.DMA((4,)),
-                pltpu.SemaphoreType.REGULAR((nf,)),
-                pltpu.SemaphoreType.REGULAR((nr,)),
+                pltpu.SemaphoreType.REGULAR((nf // 2,)),
+                pltpu.SemaphoreType.REGULAR,
+                pltpu.SemaphoreType.DMA,
                 pltpu.SemaphoreType.DMA((nf,)),
-                pltpu.SemaphoreType.DMA((nf,)),
-                pltpu.SemaphoreType.DMA((nr,)),
+                pltpu.SemaphoreType.DMA((max(nr, 4),)),
                 pltpu.SemaphoreType.DMA((nr,)),
             ],
             compiler_params=pltpu.CompilerParams(collective_id=0, has_side_effects=True,
                                                  vmem_limit_bytes=16 * 1024 * 1024),
         )(*[pltpu.with_memory_space_constraint(x.reshape(shape), pltpu.HBM)
             for x in (tile_id, pix_row, pix_col, point_value)])
-        return out.reshape(owned, quarter, LANES)
+        return jnp.sum(out, axis=0).reshape(owned, quarter, LANES)
 
     both = P(("files", "rep"))
     return jax.shard_map(per_device, mesh=mesh, in_specs=(both,) * 4,

time: 15.7 us -> 15.5 us (0.987)
  other arithmetic: 0 us -> 0.65 us
  local copies, waits for them, and re-layouts: 0.63 us -> 0 us
  Pallas kernels: 14.8 us -> 14.6 us
    reduce_sum x0 -> x1, other arithmetic: none -> 0.65 us  [per_device(): return jnp.sum(out, axis=0).reshape(owned, quarter, LANES)]
    unnamed x1 -> x0, local copies, waits for them, and re-layouts: 0.63 us -> none
where the time goes in v5:
time: 15.5 us; the launch traced here: 15.3 us
  Pallas kernels  14.6 us (94%)
  other arithmetic  0.65 us (4%)
    pallas_call x1, Pallas kernels, per_device(): pl.pallas_call(functools.partial(kernel, nf, nr, owned, quarter, cap), ou...  14.6 us
    reduce_sum x1, other arithmetic, per_device(): return jnp.sum(out, axis=0).reshape(owned, quarter, LANES)  0.65 us

profile of v5, /device:TPU:0, one launch (start us, length us, event | category | flops | bytes accessed | tf_op | source)
XLA Modules:
  0.0 15.3 jit_solution(12998983497978932739)
XLA Ops:
  0.0 14.6 %shard_map.46 = f32[4,2,64,128]{3,2,1,0:T(8,128)S(1)} custom-call(s32[32,128]{1,0:T(8,128)} %bitcast.5, s32[32,128]{1,0:T(8,128)} %bitcast.6, s32[32,128]{1,0:T(8,128)} %bitcast.7, bf16[32,128]{1,0:T(8,128)(2,1)} %bitcast.8), custom_call_target="tpu_custom_call" | custom-call | tf_op jit(solution)/shard_map/pallas_call | solution.py:225
  14.6 0.6 %reduce_sum.9 = f32[2,64,128]{2,1,0:T(8,128)} reduce(f32[4,2,64,128]{3,2,1,0:T(8,128)S(1)} %shard_map.46, f32[]{:T(128)} %constant.0.clone.1), dimensions={0}, to_apply=%region_0.0 | reduce | flops 49152 | bytes 327684 | tf_op jit(solution)/shard_map/reduce_sum | solution.py:249

commit v6 on v5

--- a/solution.py
+++ b/solution.py
@@ -12,6 +12,7 @@
 TR = 32
 TILES = 128
 SLACK = 4
+CROSS_AFTER = 5
 PAIRS = ((0, 2, 4, 6), (0, 2, 6, 4), (0, 6, 2, 4), (0, 2, 4, 6))
 MESH = pl.DeviceIdType.MESH
 BF16 = jnp.bfloat16
@@ -37,12 +38,14 @@
 
 
 def kernel(nf, nr, owned, quarter, cap, tile_ref, row_ref, col_ref, val_ref, parts,
-           tile_in, row_in, col_in, val_in, packed, got, acc,
+           tile_in, row_in, col_in, val_in, packed, got, acc, side,
            fready, rready, gsend, grecv, rsend, rrecv):
     f = lax.axis_index("files")
     r = lax.axis_index("rep")
     half = owned * quarter // 2
     band = nr * half
+    direct = nf == 8 and nr == 4
+    top = nf - 2
     blocks = tile_ref.shape[0]
     width = min(WIDE, cap)
     lines = cap // width
@@ -63,8 +66,16 @@
         pl.when(f + i < nf)(functools.partial(signal, barrier, "files", f + i))
     for i in range(1, nr):
         pl.when(r + i < nr)(functools.partial(signal, barrier, "rep", r + i))
+    if direct:
+        @pl.when(f < 2)
+        def _():
+            for to in (top, top + 1):
+                pl.semaphore_signal(barrier, inc=1, device_id={"files": to, "rep": flipped(r, 2, nr)},
+                                    device_id_type=MESH)
+    entered = f + r + (jnp.where(f >= top, 2, 0) if direct else 0)
+
     def enter():
-        pl.when(f + r > 0)(functools.partial(pl.semaphore_wait, barrier, f + r))
+        pl.when(entered > 0)(functools.partial(pl.semaphore_wait, barrier, entered))
         for i in range(1, nf):
             pl.when(f - i >= 0)(functools.partial(signal, fready.at[f // 2], "files", f - i))
         for i in range(1, nr):
@@ -139,25 +150,37 @@
             src_ref=packed.at[f], dst_ref=got.at[source], send_sem=gsend, recv_sem=grecv.at[source],
             device_id={"files": source}, device_id_type=MESH)
 
+    def cross(to):
+        return pltpu.make_async_remote_copy(
+            src_ref=packed.at[to], dst_ref=got.at[nf + f % 2], send_sem=gsend, recv_sem=grecv.at[nf + f % 2],
+            device_id={"files": to, "rep": flipped(r, 2, nr)}, device_id_type=MESH)
+
     for to in range(nf - 1):
         pl.when(to < f)(lambda to=to: send(to).start())
-
-    def add_points(chunks):
+        if direct and to == CROSS_AFTER:
+            @pl.when(f >= top)
+            def _():
+                cross(0).start()
+                cross(1).start()
+
+    def add_points(chunks, base, count):
         lhs = []
         rhs = []
         for chunk in chunks:
             cells = chunk[0:rows, :]
             row = jnp.floor(cells * (1.0 / WIDE))
             col = cells - row * WIDE
+            if count < nr:
+                row = row - (base * half).astype(jnp.float32)
             for j in range(rows):
                 row16, col16, val16 = [wide(x[j:j + 1, :]) for x in (row, col, chunk[rows:, :])]
-                lhs.append(one_hot(row16, band, [val16])[0])
+                lhs.append(one_hot(row16, count * half, [val16])[0])
                 rhs.append(one_hot(col16, WIDE, [one])[0])
         total = dot(jnp.concatenate(lhs, axis=1), jnp.concatenate(rhs, axis=1), True)
-        for q in range(nr):
+        for q in range(count):
             block = total[q * half:(q + 1) * half, :]
-            acc[q, 0] += block[:, :LANES]
-            acc[q, 1] += block[:, LANES:]
+            acc[base + q, 0] += block[:, :LANES]
+            acc[base + q, 1] += block[:, LANES:]
 
     got[f] = packed[f]
 
@@ -188,26 +211,93 @@
             k = sum(jnp.where((f // 2 == z) & (t == i), first, 0)
                     for z, order in enumerate(PAIRS) for i, first in enumerate(order))
         pair = [arrived(k), arrived(k + 1)]
-        add_points([got[source] for source in pair])
+        add_points([got[source] for source in pair], 0, nr)
         return carry
 
-    lax.fori_loop(0, nf // 2, step, 0)
+    lax.fori_loop(0, nf // 2 - (jnp.where(f < 2, 1, 0) if direct else 0), step, 0)
 
     pl.when(r < nr - 1)(functools.partial(pl.semaphore_wait, rready, nr - 1 - r))
-    backs = []
-    for k in tuple(range(2, nr)) + (1,):
-        peer = flipped(r, k, nr)
-        copy = pltpu.make_async_remote_copy(
-            src_ref=acc.at[peer], dst_ref=parts.at[k], send_sem=rsend.at[k], recv_sem=rrecv.at[k],
-            device_id={"rep": peer}, device_id_type=MESH)
-        copy.start()
-        backs.append(copy)
+    even = r % 2 == 0
+    odd = r % 2 == 1
+    sibling = flipped(r, 1, nr)
+    firsts = range(2, nr, 2)
+    seconds = range(3, nr, 2)
+
+    def pass_on(src, dst, i, to):
+        return pltpu.make_async_remote_copy(
+            src_ref=src, dst_ref=dst, send_sem=rsend.at[i], recv_sem=rrecv.at[i],
+            device_id={"rep": to}, device_id_type=MESH)
+
+    def across(k):
+        return pass_on(acc.at[flipped(r, k, nr)], parts.at[k], k, flipped(r, k, nr))
+
+    def aside(k):
+        return pass_on(acc.at[flipped(r, k + 1, nr)], side.at[k // 2 - 1], nr + k // 2 - 1, sibling)
+
+    def joined(k):
+        return pass_on(side.at[k // 2 - 1], parts.at[k], k, flipped(r, k, nr))
+
+    def join():
+        @pl.when(odd)
+        def _():
+            for k in firsts:
+                aside(k).wait_recv()
+                side[k // 2 - 1] += acc[flipped(r, k, nr)]
+                joined(k).start()
+
+    @pl.when(even)
+    def _():
+        for k in firsts:
+            across(k).start()
+            aside(k).start()
+
+    @pl.when(odd)
+    def _():
+        for k in seconds:
+            across(k).start()
+            parts[k] = jnp.zeros((2, half, LANES), jnp.float32)
+
+    if direct:
+        def late(t, carry):
+            pl.when(t == 1)(join)
+            pair = [top + 2 * t, top + 2 * t + 1]
+            for source in pair:
+                pltpu.make_async_remote_copy(
+                    src_ref=packed.at[f], dst_ref=got.at[source], send_sem=gsend, recv_sem=grecv.at[source],
+                    device_id={"files": (f + 1) % nf}, device_id_type=MESH).wait_recv()
+            add_points([got[source] for source in pair], (r // 2) * 2, 2)
+            return carry
+
+        lax.fori_loop(0, jnp.where(f < 2, 2, 0), late, 0)
+        pl.when(f >= 2)(join)
+    else:
+        join()
+    across(1).start()
     parts[0] = acc[r]
     pltpu.make_async_remote_copy(
         src_ref=packed.at[pl.ds(0, nf - 1)], dst_ref=got.at[pl.ds(0, nf - 1)], send_sem=gsend, recv_sem=grecv.at[0],
         device_id={"files": f}, device_id_type=MESH).wait_send()
-    for copy in backs:
-        copy.wait()
+    if direct:
+        @pl.when(f >= top)
+        def _():
+            pltpu.make_async_remote_copy(
+                src_ref=packed.at[pl.ds(0, 2)], dst_ref=got.at[pl.ds(0, 2)], send_sem=gsend,
+                recv_sem=grecv.at[0], device_id={"files": f}, device_id_type=MESH).wait_send()
+    across(1).wait()
+    for k in firsts:
+        across(k).wait()
+
+    @pl.when(even)
+    def _():
+        for k in firsts:
+            aside(k).wait_send()
+        for k in seconds:
+            across(k).wait_recv()
+
+    @pl.when(odd)
+    def _():
+        for k in seconds:
+            across(k).wait_send()
 
 
 def solution(mesh):
@@ -233,14 +323,15 @@
                 pltpu.VMEM(shape, jnp.int32),
                 pltpu.VMEM(shape, point_value.dtype),
                 pltpu.VMEM((nf, message, LANES), jnp.float32),
-                pltpu.VMEM((nf, message, LANES), jnp.float32),
+                pltpu.VMEM((nf + 2, message, LANES), jnp.float32),
                 pltpu.VMEM((nr, 2, half, LANES), jnp.float32),
+                pltpu.VMEM((nr // 2 - 1, 2, half, LANES), jnp.float32),
                 pltpu.SemaphoreType.REGULAR((nf // 2,)),
                 pltpu.SemaphoreType.REGULAR,
                 pltpu.SemaphoreType.DMA,
-                pltpu.SemaphoreType.DMA((nf,)),
-                pltpu.SemaphoreType.DMA((max(nr, 4),)),
-                pltpu.SemaphoreType.DMA((nr,)),
+                pltpu.SemaphoreType.DMA((nf + 2,)),
+                pltpu.SemaphoreType.DMA((nr + nr // 2 - 1,)),
+                pltpu.SemaphoreType.DMA((nr + nr // 2 - 1,)),
             ],
             compiler_params=pltpu.CompilerParams(collective_id=0, has_side_effects=True,
                                                  vmem_limit_bytes=16 * 1024 * 1024),

time: 15.5 us -> 15.3 us (0.987)
  no operation moved by 1% of the time
where the time goes in v6:
time: 15.3 us; the launch traced here: 15.1 us
  Pallas kernels  14.5 us (95%)
  other arithmetic  0.65 us (4%)
    pallas_call x1, Pallas kernels, per_device(): pl.pallas_call(functools.partial(kernel, nf, nr, owned, quarter, cap), ou...  14.5 us
    reduce_sum x1, other arithmetic, per_device(): return jnp.sum(out, axis=0).reshape(owned, quarter, LANES)  0.65 us

profile of v6, /device:TPU:0, one launch (start us, length us, event | category | flops | bytes accessed | tf_op | source)
XLA Modules:
  0.0 15.1 jit_solution(7044480908051105537)
XLA Ops:
  0.0 14.5 %shard_map.46 = f32[4,2,64,128]{3,2,1,0:T(8,128)S(1)} custom-call(s32[32,128]{1,0:T(8,128)} %bitcast.5, s32[32,128]{1,0:T(8,128)} %bitcast.6, s32[32,128]{1,0:T(8,128)} %bitcast.7, bf16[32,128]{1,0:T(8,128)(2,1)} %bitcast.8), custom_call_target="tpu_custom_call" | custom-call | tf_op jit(solution)/shard_map/pallas_call | solution.py:315
  14.5 0.6 %reduce_sum.9 = f32[2,64,128]{2,1,0:T(8,128)} reduce(f32[4,2,64,128]{3,2,1,0:T(8,128)S(1)} %shard_map.46, f32[]{:T(128)} %constant.0.clone.1), dimensions={0}, to_apply=%region_0.0 | reduce | flops 49152 | bytes 327684 | tf_op jit(solution)/shard_map/reduce_sum | solution.py:340

commit v7 on v6

--- a/solution.py
+++ b/solution.py
@@ -12,7 +12,7 @@
 TR = 32
 TILES = 128
 SLACK = 4
-CROSS_AFTER = 5
+CROSS_AFTER = (1, 5)
 PAIRS = ((0, 2, 4, 6), (0, 2, 6, 4), (0, 6, 2, 4), (0, 2, 4, 6))
 MESH = pl.DeviceIdType.MESH
 BF16 = jnp.bfloat16
@@ -157,11 +157,8 @@
 
     for to in range(nf - 1):
         pl.when(to < f)(lambda to=to: send(to).start())
-        if direct and to == CROSS_AFTER:
-            @pl.when(f >= top)
-            def _():
-                cross(0).start()
-                cross(1).start()
+        if direct and to in CROSS_AFTER:
+            pl.when(f >= top)(lambda to=to: cross(CROSS_AFTER.index(to)).start())
 
     def add_points(chunks, base, count):
         lhs = []

time: 15.3 us -> 15 us (0.980)
  the two profiles are of different devices: /device:TPU:0 before, /device:TPU:13 now
where the time goes in v7:
time: 15 us; the launch traced here: 14.8 us
  Pallas kernels  14.2 us (95%)
  other arithmetic  0.65 us (4%)
    pallas_call x1, Pallas kernels, per_device(): pl.pallas_call(functools.partial(kernel, nf, nr, owned, quarter, cap), ou...  14.2 us
    reduce_sum x1, other arithmetic, per_device(): return jnp.sum(out, axis=0).reshape(owned, quarter, LANES)  0.65 us

profile of v7, /device:TPU:13, one launch (start us, length us, event | category | flops | bytes accessed | tf_op | source)
XLA Modules:
  0.0 14.8 jit_solution(15149214827797358903)
XLA Ops:
  0.0 14.2 %shard_map.46 = f32[4,2,64,128]{3,2,1,0:T(8,128)S(1)} custom-call(s32[32,128]{1,0:T(8,128)} %bitcast.5, s32[32,128]{1,0:T(8,128)} %bitcast.6, s32[32,128]{1,0:T(8,128)} %bitcast.7, bf16[32,128]{1,0:T(8,128)(2,1)} %bitcast.8), custom_call_target="tpu_custom_call" | custom-call | tf_op jit(solution)/shard_map/pallas_call | solution.py:312
  14.2 0.6 %reduce_sum.9 = f32[2,64,128]{2,1,0:T(8,128)} reduce(f32[4,2,64,128]{3,2,1,0:T(8,128)S(1)} %shard_map.46, f32[]{:T(128)} %constant.0.clone.1), dimensions={0}, to_apply=%region_0.0 | reduce | flops 49152 | bytes 327684 | tf_op jit(solution)/shard_map/reduce_sum | solution.py:337

commit v8 on v7

--- a/solution.py
+++ b/solution.py
@@ -13,6 +13,7 @@
 TILES = 128
 SLACK = 4
 CROSS_AFTER = (1, 5)
+EARLY = (0, 2, 1, 3)
 PAIRS = ((0, 2, 4, 6), (0, 2, 6, 4), (0, 6, 2, 4), (0, 2, 4, 6))
 MESH = pl.DeviceIdType.MESH
 BF16 = jnp.bfloat16
@@ -156,7 +157,8 @@
             device_id={"files": to, "rep": flipped(r, 2, nr)}, device_id_type=MESH)
 
     for to in range(nf - 1):
-        pl.when(to < f)(lambda to=to: send(to).start())
+        turn = jnp.where(f >= 4, EARLY[to], to) if direct and to < 4 else to
+        pl.when(turn < f)(lambda turn=turn: send(turn).start())
         if direct and to in CROSS_AFTER:
             pl.when(f >= top)(lambda to=to: cross(CROSS_AFTER.index(to)).start())
 

time: 15 us -> 15 us (level)
  no operation moved by 1% of the time
where the time goes in v8:
time: 15 us; the launch traced here: 14.8 us
  Pallas kernels  14.2 us (95%)
  other arithmetic  0.65 us (4%)
    pallas_call x1, Pallas kernels, per_device(): pl.pallas_call(functools.partial(kernel, nf, nr, owned, quarter, cap), ou...  14.2 us
    reduce_sum x1, other arithmetic, per_device(): return jnp.sum(out, axis=0).reshape(owned, quarter, LANES)  0.65 us

profile of v8, /device:TPU:13, one launch (start us, length us, event | category | flops | bytes accessed | tf_op | source)
XLA Modules:
  0.0 14.8 jit_solution(7142297571283233664)
XLA Ops:
  0.0 14.2 %shard_map.46 = f32[4,2,64,128]{3,2,1,0:T(8,128)S(1)} custom-call(s32[32,128]{1,0:T(8,128)} %bitcast.5, s32[32,128]{1,0:T(8,128)} %bitcast.6, s32[32,128]{1,0:T(8,128)} %bitcast.7, bf16[32,128]{1,0:T(8,128)(2,1)} %bitcast.8), custom_call_target="tpu_custom_call" | custom-call | tf_op jit(solution)/shard_map/pallas_call | solution.py:314
  14.2 0.6 %reduce_sum.9 = f32[2,64,128]{2,1,0:T(8,128)} reduce(f32[4,2,64,128]{3,2,1,0:T(8,128)S(1)} %shard_map.46, f32[]{:T(128)} %constant.0.clone.1), dimensions={0}, to_apply=%region_0.0 | reduce | flops 49152 | bytes 327684 | tf_op jit(solution)/shard_map/reduce_sum | solution.py:339
